TPU v7x, 32 devices: a whole 2x2x4 slice. The times are simulated.
32 devices in a mesh: seq: 4 (over x, core), tensor: 8 (over z, y).
Axes of the slice: x: 2, y: 2, z: 4, core: 2. Of those that a mesh axis runs over, the one named last changes fastest.
Arguments:
- token_ids: int32 [2, 7], replicated, may hold values from 0 to 131071
- cache_lengths: int32 [7], replicated, may hold values from 1 to 5118
- embed_table: bfloat16 [131072, 1024], P('seq', 'tensor'), may hold values from -64 to 64
- attn_gain: float32 [1024], replicated, may hold values from 0.1 to 1.9
- final_gain: float32 [1024], replicated, may hold values from 0.1 to 1.9
- w_qkv: bfloat16 [1024, 3, 1024], P(None, None, 'tensor'), may hold values from -0.1875 to 0.1875
- w_out: bfloat16 [1024, 1024], P('tensor'), may hold values from -0.1875 to 0.1875
- cache_keys: bfloat16 [7, 5120, 1024], P(None, 'seq', 'tensor'), may hold values from -300 to 300
- cache_values: bfloat16 [7, 5120, 1024], P(None, 'seq', 'tensor'), may hold values from -24 to 24
Outputs:
- hidden: bfloat16 [2, 7, 1024], P(None, None, 'tensor')
- new_kv: bfloat16 [2, 2, 7, 1024], P(None, None, None, 'tensor')
- logprobs: float32 [2, 7, 131072], P(None, None, ('seq', 'tensor'))
All inputs are finite; a program needn't handle non-finite values.
Results may differ from a plain program's by a relative error of at most 0.0085.
The roundings to bfloat16 on the way count: a program that leaves them out, or rounds other values in their place, can miss the bound.
Values may be sent and summed in bfloat16 or wider, within the bound.
A program may use at most 64 MiB of HBM per device.

v0:
```python
import math
import jax
import jax.numpy as jnp
from jax import lax
from jax.sharding import PartitionSpec as P

HD = 128
epsilon = 1e-05
logit_gain = 2.0


def combined_all(value, axis, join):
    pieces = jax.tree.map(lambda part: lax.all_gather(part, axis), value)
    head = jax.tree.map(lambda part: part[0], pieces)
    tail = jax.tree.map(lambda part: part[1:], pieces)
    running, _ = lax.scan(lambda running, share: (join(running, share), None), head, tail)
    return running


def rotate(vector, positions):
    half_size = vector.shape[-1] // 2
    frequency = 10000.0 ** (-(jnp.arange(half_size, dtype=jnp.float32) * 2.0 / vector.shape[-1]))
    angles = positions.astype(jnp.float32)[..., None] * frequency
    cosine_term = jnp.cos(angles)[:, :, None, :]
    sine_term = jnp.sin(angles)[:, :, None, :]
    first_half = vector[..., :half_size]
    second_half = vector[..., half_size:]
    return jnp.concatenate(
        [
            first_half * cosine_term - second_half * sine_term,
            first_half * sine_term + second_half * cosine_term,
        ],
        -1,
    )


def pair_join(earlier, later):
    highest = jnp.maximum(earlier[0], later[0])
    return (
        highest,
        earlier[1] * jnp.exp(earlier[0] - highest) + later[1] * jnp.exp(later[0] - highest),
    )


def body(
    token_ids,
    cache_lengths,
    embed_table,
    attn_gain,
    final_gain,
    w_qkv,
    w_out,
    cache_keys,
    cache_values,
):
    streams = token_ids.shape[1]
    vocab_rows, local_width = embed_table.shape
    model_width = attn_gain.shape[0]
    heads_here = local_width // HD
    slot_count = cache_keys.shape[1]
    seq_index = lax.axis_index("seq")
    tensor_index = lax.axis_index("tensor")
    local_ids = token_ids - seq_index * vocab_rows
    inside = (local_ids >= 0) & (local_ids < vocab_rows)
    picked = embed_table[jnp.clip(local_ids, 0, vocab_rows - 1)]
    picked = jnp.where(inside[..., None], picked, jnp.zeros_like(picked))
    embed_local = lax.psum(picked.astype(jnp.float32).astype(jnp.bfloat16), "seq").astype(
        jnp.float32
    )
    embed_whole = lax.all_gather(
        embed_local.astype(jnp.bfloat16), "tensor", axis=2, tiled=True
    ).astype(jnp.float32)
    normed = (
        embed_whole
        * lax.rsqrt(jnp.mean(embed_whole * embed_whole, -1, keepdims=True) + epsilon)
        * attn_gain
    ).astype(jnp.bfloat16)
    projected = jnp.einsum("sbd,dcf->sbcf", normed, w_qkv, preferred_element_type=jnp.float32)
    head_shape = (2, streams, heads_here, HD)
    positions = cache_lengths[None, :] + jnp.arange(2, dtype=jnp.int32)[:, None]
    queries = rotate(projected[:, :, 0].reshape(head_shape), positions).astype(jnp.bfloat16)
    new_keys = rotate(projected[:, :, 1].reshape(head_shape), positions).astype(jnp.bfloat16)
    new_values = projected[:, :, 2].reshape(head_shape).astype(jnp.bfloat16)
    new_kv = jnp.stack(
        [new_keys.reshape(2, streams, local_width), new_values.reshape(2, streams, local_width)]
    )
    inverse = HD ** (-0.5)
    key_rows = cache_keys.reshape(streams, slot_count, heads_here, HD)
    value_rows = cache_values.reshape(streams, slot_count, heads_here, HD)
    scores = (
        jnp.einsum("sbhe,bjhe->sbhj", queries, key_rows, preferred_element_type=jnp.float32)
        * inverse
    )
    slot_positions = seq_index * slot_count + jnp.arange(slot_count, dtype=jnp.int32)
    visible = (slot_positions[None, :] < cache_lengths[:, None])[None, :, None, :]
    local_max = jnp.max(jnp.where(visible, scores, -1e30), -1)
    weights = jnp.where(visible, jnp.exp(scores - local_max[..., None]), 0.0)
    local_sum = jnp.sum(weights, -1)
    local_out = jnp.einsum(
        "sbhj,bjhe->sbhe",
        weights,
        value_rows,
        preferred_element_type=jnp.float32,
        precision=lax.Precision.HIGHEST,
    )
    highest = lax.pmax(local_max, "seq")
    factor = jnp.exp(local_max - highest)
    cache_total, cache_out = lax.psum((local_sum * factor, local_out * factor[..., None]), "seq")
    fresh_scores = (
        jnp.einsum("sbhe,tbhe->sbht", queries, new_keys, preferred_element_type=jnp.float32)
        * inverse
    )
    allowed = (jnp.arange(2)[None, :] <= jnp.arange(2)[:, None])[:, None, None, :]
    fresh_max = jnp.max(jnp.where(allowed, fresh_scores, -1e30), -1)
    overall = jnp.maximum(highest, fresh_max)
    fresh_weights = jnp.where(allowed, jnp.exp(fresh_scores - overall[..., None]), 0.0)
    cache_scale = jnp.exp(highest - overall)
    denominator = cache_total * cache_scale + jnp.sum(fresh_weights, -1)
    numerator = cache_out * cache_scale[..., None] + jnp.einsum(
        "sbht,tbhe->sbhe",
        fresh_weights,
        new_values,
        preferred_element_type=jnp.float32,
        precision=lax.Precision.HIGHEST,
    )
    attended = (
        (numerator / denominator[..., None]).astype(jnp.bfloat16).reshape(2 * streams, local_width)
    )
    mixed_rows = jnp.dot(attended, w_out, preferred_element_type=jnp.float32).reshape(
        2, streams, model_width
    )
    mixed_local = lax.psum_scatter(mixed_rows, "tensor", scatter_dimension=2, tiled=True)
    hidden = (embed_local + mixed_local).astype(jnp.bfloat16)
    hidden_float = hidden.astype(jnp.float32)
    final_squares = lax.psum(jnp.sum(hidden_float * hidden_float, -1), "tensor")
    factor_rows = (
        lax.rsqrt(final_squares / model_width + epsilon) * (logit_gain / math.sqrt(model_width))
    ).reshape(2 * streams, 1)
    final_local = lax.dynamic_slice_in_dim(final_gain, tensor_index * local_width, local_width)
    gated_rows = (hidden_float * final_local).astype(jnp.bfloat16).reshape(2 * streams, local_width)
    partial_logits = lax.dot_general(
        gated_rows, embed_table, (((1,), (1,)), ((), ())), preferred_element_type=jnp.float32
    )
    shares = (
        lax.psum_scatter(partial_logits, "tensor", scatter_dimension=1, tiled=True) * factor_rows
    )
    share_max = jnp.max(shares, -1)
    share_sum = jnp.sum(jnp.exp(shares - share_max[:, None]), -1)
    vocab_max, vocab_sum = combined_all((share_max, share_sum), ("seq", "tensor"), pair_join)
    logprobs = shares - (vocab_max + jnp.log(vocab_sum))[:, None]
    return (hidden, new_kv, logprobs.reshape(2, streams, -1))


def solution(mesh):
    in_specs = (
        P(),
        P(),
        P("seq", "tensor"),
        P(),
        P(),
        P(None, None, "tensor"),
        P("tensor", None),
        P(None, "seq", "tensor"),
        P(None, "seq", "tensor"),
    )
    out_specs = (
        P(None, None, "tensor"),
        P(None, None, None, "tensor"),
        P(None, None, ("seq", "tensor")),
    )
    return jax.shard_map(body, mesh=mesh, in_specs=in_specs, out_specs=out_specs, check_vma=False)
```

profile of v0, /device:TPU:0, one launch (start us, length us, event | category | flops | bytes accessed | tf_op | source)
XLA Modules:
  0.0 251.6 jit_solution(10912633208323982474)
XLA Ops:
  7.2 0.8 compare_select_fusion
  8.1 0.7 compare_and_fusion
  8.8 0.7 add_convert_fusion.1
  9.5 0.7 broadcast_compare_fusion
  10.2 0.1 reshape.222
  10.3 5.0 %gather_fusion = bf16[14,128]{1,0:T(8,128)(2,1)S(1)} fusion(bf16[32768,128]{1,0:T(8,128)(2,1)} %param.13, s32[1024]{0:T(1024)S(1)} %pad_clamp_fusion), kind=kCustom, calls=%fused_computation | custom fusion | bytes 7224 | tf_op jit(solution)/shard_map/gather | solution.py:65
  15.4 8.3 %psum.28 = bf16[2,7,128]{2,1,0:T(8,128)(2,1)S(1)} all-reduce(bf16[2,7,128]{2,1,0:T(8,128)(2,1)S(1)} %broadcast_select_fusion), channel_id=1, replica_groups=mesh['seq'=4,'tensor'=8] {'seq'}, use_global_device_ids=true, to_apply=%region_0.1 | all-reduce | flops 1792 | bytes 7168 | tf_op jit(solution)/shard_map/psum | solution.py:67
  23.7 26.4 %all_gather.15 = bf16[2,7,1024]{2,1,0:T(8,128)(2,1)S(1)} all-gather(bf16[2,7,128]{2,1,0:T(8,128)(2,1)S(1)} %psum.28), channel_id=1, replica_groups=mesh['seq'=4,'tensor'=8] {'tensor'}, dimensions={2}, use_global_device_ids=true | all-gather | bytes 32256 | tf_op jit(solution)/shard_map/all_gather | solution.py:70
  50.1 0.1 fusion.16
  50.2 1.4 fusion.11
  51.6 0.1 fusion.39
  51.8 0.1 pad_maximum_fusion.1
  51.8 0.8 select_reduce_fusion
  52.6 0.1 copy.53
  52.7 0.2 fusion.23
  53.0 0.1 copy.64
  53.1 5.8 %pmax.7 = f32[2,7,1]{1,0,2:T(2,128)S(1)} all-reduce(f32[2,7,1]{1,0,2:T(2,128)S(1)} %bitcast.154), channel_id=1, replica_groups=mesh['seq'=4,'tensor'=8] {'seq'}, use_global_device_ids=true, to_apply=%region_3.4 | all-reduce | flops 14 | bytes 112 | tf_op jit(solution)/shard_map/pmax | solution.py:106
  58.9 0.1 convolution_multiply_fusion.1
  59.0 0.1 copy.59
  59.1 0.1 fusion.47
  59.3 0.1 copy.63
  59.4 0.1 copy.54
  59.5 2.7 %fusion.6 = f32[2,7,1,128]{3,0,1,2:T(2,128)S(1)} fusion(bf16[7,1280,128]{2,1,0:T(8,128)(2,1)} %param.19, f32[2,7,1,1280]{3,0,1,2:T(2,128)S(1)} %get-tuple-element.74, pred[7,1280]{1,0:T(8,128)(4,1)S(1)} %broadcast_compare_fusion, f32[2,7]{0,1:T(8,128)S(1)} %get-tuple-element.73, f32[2,7]{0,1:T(8,128)S(1)} %copy.54), kind=kOutput, calls=%fused_computation.12 | convolution fusion | flops 27562752 | bytes 2381680 | tf_op jit(solution)/shard_map/sbhj,bjhe->sbhe/dot_general | solution.py:99
  62.2 5.8 %all-reduce.3 = (f32[2,7,1,128]{3,0,1,2:T(2,128)S(1)}, f32[2,7,1]{1,0,2:T(2,128)S(1)}) all-reduce(f32[2,7,1,128]{3,0,1,2:T(2,128)S(1)} %fusion.6, f32[2,7,1]{1,0,2:T(2,128)S(1)} %get-tuple-element.70), channel_id=1, replica_groups=mesh['seq'=4,'tensor'=8] {'seq'}, use_global_device_ids=true, to_apply=%region_4.5 | all-reduce | flops 1806 | bytes 14448 | tf_op jit(solution)/shard_map/psum | solution.py:108
  68.1 0.1 copy.65
  68.2 0.1 copy.60
  68.3 0.2 fusion.10
  68.4 0.8 fusion.13
  69.3 0.8 dynamic_slice.10
  70.1 53.2 %reduce-scatter.3.cloned.1.call-done = f32[2,7,128]{2,1,0:T(8,128)} async-done(((f32[2,7,1024]{2,1,0:T(8,128)}), f32[2,7,128]{2,1,0:T(8,128)}) %reduce-scatter.3.cloned.1.call-update) | async-done | bytes 7184 | tf_op jit(solution)/shard_map/reduce_scatter | solution.py:132
  123.3 0.8 fusion.33
  124.1 7.0 %fusion.62 = f32[14,32768]{1,0:T(8,128)} fusion(bf16[14,128]{1,0:T(8,128)(2,1)S(1)} %reshape.218, bf16[32768,128]{1,0:T(8,128)(2,1)} %param.13), kind=kOutput, calls=%fused_computation.106 | convolution fusion | flops 117440512 | bytes 10227200 | tf_op jit(solution)/shard_map/dot_general | solution.py:141
  131.1 0.1 pad_maximum_fusion
  131.2 0.6 copy.68
  131.8 19.6 %psum.31 = f32[2,7]{1,0:T(2,128)S(1)} all-reduce(f32[2,7]{1,0:T(2,128)S(1)} %get-tuple-element.58), channel_id=1, replica_groups=mesh['seq'=4,'tensor'=8] {'tensor'}, use_global_device_ids=true, to_apply=%region_12.13 | all-reduce | flops 14 | bytes 112 | tf_op jit(solution)/shard_map/psum | solution.py:135
  151.4 0.6 copy.67
  152.0 0.1 mul.205
  152.1 46.9 %reduce-scatter.5.cloned.1.call-done = f32[14,4096]{1,0:T(8,128)} async-done(((f32[14,32768]{1,0:T(8,128)}), f32[14,4096]{1,0:T(8,128)}) %reduce-scatter.5.cloned.1.call-update) | async-done | bytes 229392 | tf_op jit(solution)/shard_map/reduce_scatter | solution.py:145
  199.0 1.2 multiply_reduce_fusion
  200.2 0.2 dynamic-update-slice
  200.4 1.2 exponential_reduce_fusion
  201.6 0.2 dynamic-update-slice.1
  201.9 39.3 %all-reduce.2 = (f32[448]{0:T(512)S(1)}, f32[448]{0:T(512)S(1)}) all-reduce(f32[448]{0:T(512)S(1)} %dynamic-update-slice, f32[448]{0:T(512)S(1)} %dynamic-update-slice.1), channel_id=2, replica_groups=mesh['seq'=4,'tensor'=8] {'seq','tensor'}, use_global_device_ids=true, to_apply=%add | all-reduce | flops 896 | bytes 7168
  241.4 0.1 reshape.236
  241.4 0.1 reshape.237
  241.6 1.2 while.12
  242.8 1.0 multiply_subtract_fusion
  243.9 0.9 copy.69
  (61 shorter events, 1.4 us)
Async XLA Ops:
  7.2 44.7 %copy-start = (bf16[7,1280,128]{2,1,0:T(8,128)(2,1)S(1)}, bf16[7,1280,128]{2,1,0:T(8,128)(2,1)}, u32[]{:S(2)}) copy-start(bf16[7,1280,128]{2,1,0:T(8,128)(2,1)} %param.18) | copy-start | bytes 6881284
  7.2 116.1 %reduce-scatter.3.cloned.1.call-start = ((), (), s32[]{:S(2)}) async-start(), calls=%async_computation.2 | async-start | bytes 73728 | tf_op jit(solution)/shard_map/reduce_scatter | solution.py:132
  51.8 16.6 %copy-start.1 = (bf16[128,1024]{1,0:T(8,128)(2,1)S(1)}, bf16[128,1024]{1,0:T(8,128)(2,1)}, u32[]{:S(2)}) copy-start(bf16[128,1024]{1,0:T(8,128)(2,1)} %param.17) | copy-start | bytes 786436
  69.3 129.8 %reduce-scatter.5.cloned.1.call-start = ((), (), s32[]{:S(2)}) async-start(), calls=%async_computation.3 | async-start | bytes 2359296 | tf_op jit(solution)/shard_map/reduce_scatter | solution.py:145
Sparse Core Ops, SparseCore 0:
  69.4 53.8 reduce-scatter.2
  131.3 67.7 reduce-scatter.4
where the time goes:
time: 252 us
  blocking collectives  105 us (42%)
  waiting for transfers between devices  100 us (40%)
  between operations  14.2 us (6%)
  matrix products  13 us (5%)
  local copies, waits for them, and re-layouts  9.57 us (4%)
  other arithmetic  8.84 us (4%)
    reduce_scatter x1, waiting for transfers between devices, body(): lax.psum_scatter(mixed_rows, 'tensor', scatter_dimension=2, tiled=True)  53.2 us
    reduce_scatter x1, waiting for transfers between devices, body(): lax.psum_scatter(partial_logits, 'tensor', scatter_dimension=1, tiled=True)  46.9 us
    unnamed x1, blocking collectives  39.3 us
    all_gather x1, blocking collectives, body(): lax.all_gather(embed_local.astype(jnp.bfloat16), 'tensor', axis=2, tiled=...  26.4 us
    psum x1, blocking collectives, body(): final_squares = lax.psum(jnp.sum(hidden_float * hidden_float, -1), 'tensor')  19.6 us
    psum x1, blocking collectives, body(): lax.psum(picked.astype(jnp.float32).astype(jnp.bfloat16), 'seq')  8.35 us
    dot_general x1, matrix products, body(): lax.dot_general(gated_rows, embed_table, (((1,), (1,)), ((), ())), prefer...  7.03 us
    pmax x1, blocking collectives, body(): highest = lax.pmax(local_max, 'seq')  5.85 us
  transfers between devices with their start and end apart: 2, of which 2 were waited for; matrix products, arithmetic and copies ran while one was open for 1% of the time, Pallas kernels for 0%

commit v1 on v0

--- a/solution.py
+++ b/solution.py
@@ -67,9 +67,17 @@
     embed_local = lax.psum(picked.astype(jnp.float32).astype(jnp.bfloat16), "seq").astype(
         jnp.float32
     )
-    embed_whole = lax.all_gather(
-        embed_local.astype(jnp.bfloat16), "tensor", axis=2, tiled=True
-    ).astype(jnp.float32)
+
+    def _match_digits(target, dimension_no):
+        after = jnp.concatenate(
+            lax.all_to_all(
+                jnp.stack([target for _ in range(lax.axis_size("tensor"))]), "tensor", 0, 0
+            ),
+            axis=dimension_no,
+        )
+        return after
+
+    embed_whole = _match_digits(embed_local.astype(jnp.bfloat16), 2).astype(jnp.float32)
     normed = (
         embed_whole
         * lax.rsqrt(jnp.mean(embed_whole * embed_whole, -1, keepdims=True) + epsilon)

time: 252 us -> 236 us (0.937)
  blocking collectives: 105 us -> 79.1 us
  starting transfers between devices: 0.08 us -> 5.91 us
  waiting for transfers between devices: 100 us -> 103 us
    all_gather x1 -> x0, blocking collectives: 26.4 us -> none  [body(): lax.all_gather(embed_local.astype(jnp.bfloat16), 'tensor', axis=2, tiled=...]
    all_to_all x0 -> x1, starting transfers between devices: none -> 5.83 us  [_match_digits(): lax.all_to_all(jnp.stack([target for _ in range(lax.axis_size('tensor'))]...]
    all_to_all x0 -> x1, waiting for transfers between devices: none -> 5.18 us  [_match_digits(): lax.all_to_all(jnp.stack([target for _ in range(lax.axis_size('tensor'))]...]
  transfers between devices with their start and end apart: 2 -> 3, of which waited for: 2 -> 3; matrix products, arithmetic and copies ran while one was open for 1% -> 2% of each run, Pallas kernels for 0% -> 0%
where the time goes in v1:
time: 236 us
  waiting for transfers between devices  103 us (44%)
  blocking collectives  79.1 us (34%)
  between operations  14.2 us (6%)
  matrix products  13 us (6%)
  local copies, waits for them, and re-layouts  10.5 us (4%)
  other arithmetic  9.67 us (4%)
  starting transfers between devices  5.91 us (3%)
    reduce_scatter x1, waiting for transfers between devices, body(): lax.psum_scatter(mixed_rows, 'tensor', scatter_dimension=2, tiled=True)  51.1 us
    reduce_scatter x1, waiting for transfers between devices, body(): lax.psum_scatter(partial_logits, 'tensor', scatter_dimension=1, tiled=True)  46.6 us
    unnamed x1, blocking collectives  39.5 us
    psum x1, blocking collectives, body(): final_squares = lax.psum(jnp.sum(hidden_float * hidden_float, -1), 'tensor')  19.6 us
    psum x1, blocking collectives, body(): lax.psum(picked.astype(jnp.float32).astype(jnp.bfloat16), 'seq')  8.35 us
    dot_general x1, matrix products, body(): lax.dot_general(gated_rows, embed_table, (((1,), (1,)), ((), ())), prefer...  7.03 us
    pmax x1, blocking collectives, body(): highest = lax.pmax(local_max, 'seq')  5.85 us
    psum x1, blocking collectives, body(): lax.psum((local_sum * factor, local_out * factor[..., None]), 'seq')  5.85 us
  transfers between devices with their start and end apart: 3, of which 3 were waited for; matrix products, arithmetic and copies ran while one was open for 2% of the time, Pallas kernels for 0%

profile of v1, /device:TPU:0, one launch (start us, length us, event | category | flops | bytes accessed | tf_op | source)
XLA Modules:
  0.0 235.8 jit_solution(16338843730519222198)
XLA Ops:
  7.2 0.8 compare_select_fusion
  8.0 0.7 compare_and_fusion
  8.8 5.0 %gather_fusion = bf16[14,128]{1,0:T(8,128)(2,1)S(1)} fusion(bf16[32768,128]{1,0:T(8,128)(2,1)} %param.13, s32[1024]{0:T(1024)S(1)} %pad_clamp_fusion), kind=kCustom, calls=%fused_computation | custom fusion | bytes 7224 | tf_op jit(solution)/shard_map/gather | solution.py:65
  13.9 8.3 %psum.28 = bf16[2,7,128]{2,1,0:T(8,128)(2,1)S(1)} all-reduce(bf16[2,7,128]{2,1,0:T(8,128)(2,1)S(1)} %broadcast_select_fusion), channel_id=1, replica_groups=mesh['seq'=4,'tensor'=8] {'seq'}, use_global_device_ids=true, to_apply=%region_0.1 | all-reduce | flops 1792 | bytes 7168 | tf_op jit(solution)/shard_map/psum | solution.py:67
  22.3 0.6 stack.4
  22.9 5.8 %all-to-all-start = ((bf16[8,2,7,128]{3,1,2,0:T(2,128)(2,1)}), bf16[8,2,7,128]{3,1,2,0:T(2,128)(2,1)S(1)}, u32[]{:S(2)}, u32[]{:S(2)}) async-start(bf16[8,2,7,128]{3,1,2,0:T(2,128)(2,1)} %stack.4), calls=%async_computation | async-start | bytes 57344 | tf_op jit(solution)/shard_map/all_to_all | solution.py:73
  28.8 0.7 add_convert_fusion.1
  29.5 0.7 broadcast_compare_fusion
  30.2 5.2 %all-to-all-done = bf16[8,2,7,128]{3,1,2,0:T(2,128)(2,1)S(1)} async-done(((bf16[8,2,7,128]{3,1,2,0:T(2,128)(2,1)}), bf16[8,2,7,128]{3,1,2,0:T(2,128)(2,1)S(1)}, u32[]{:S(2)}, u32[]{:S(2)}) %all-to-all-start) | async-done | bytes 28704 | tf_op jit(solution)/shard_map/all_to_all | solution.py:73
  35.4 0.1 fusion.16
  35.5 0.1 copy.137
  35.7 0.8 fusion.20
  36.5 1.4 fusion.11
  37.8 0.1 fusion.37
  38.0 0.8 select_reduce_fusion
  38.8 0.1 copy.112
  38.9 0.2 fusion.21
  39.2 0.1 copy.123
  39.3 5.8 %pmax.7 = f32[2,7,1]{1,0,2:T(2,128)S(1)} all-reduce(f32[2,7,1]{1,0,2:T(2,128)S(1)} %bitcast.155), channel_id=1, replica_groups=mesh['seq'=4,'tensor'=8] {'seq'}, use_global_device_ids=true, to_apply=%region_3.4 | all-reduce | flops 14 | bytes 112 | tf_op jit(solution)/shard_map/pmax | solution.py:114
  45.1 0.1 convolution_multiply_fusion.1
  45.2 0.1 copy.118
  45.5 0.1 copy.122
  45.6 0.1 copy.113
  45.7 2.7 %fusion.6 = f32[2,7,1,128]{3,0,1,2:T(2,128)S(1)} fusion(bf16[7,1280,128]{2,1,0:T(8,128)(2,1)} %param.19, f32[2,7,1,1280]{3,0,1,2:T(2,128)S(1)} %get-tuple-element.80, pred[7,1280]{1,0:T(8,128)(4,1)S(1)} %broadcast_compare_fusion, f32[2,7]{0,1:T(8,128)S(1)} %get-tuple-element.79, f32[2,7]{0,1:T(8,128)S(1)} %copy.113), kind=kOutput, calls=%fused_computation.12 | convolution fusion | flops 27562752 | bytes 2381680 | tf_op jit(solution)/shard_map/sbhj,bjhe->sbhe/dot_general | solution.py:107
  48.4 5.8 %all-reduce.3 = (f32[2,7,1,128]{3,0,1,2:T(2,128)S(1)}, f32[2,7,1]{1,0,2:T(2,128)S(1)}) all-reduce(f32[2,7,1,128]{3,0,1,2:T(2,128)S(1)} %fusion.6, f32[2,7,1]{1,0,2:T(2,128)S(1)} %get-tuple-element.76), channel_id=1, replica_groups=mesh['seq'=4,'tensor'=8] {'seq'}, use_global_device_ids=true, to_apply=%region_4.5 | all-reduce | flops 1806 | bytes 14448 | tf_op jit(solution)/shard_map/psum | solution.py:116
  54.3 0.1 copy.124
  54.4 0.1 copy.119
  54.5 0.2 fusion.10
  54.6 0.8 fusion.13
  55.5 0.8 dynamic_slice.10
  56.3 51.1 %reduce-scatter.3.cloned.1.call-done = f32[2,7,128]{2,1,0:T(8,128)} async-done(((f32[2,7,1024]{2,1,0:T(8,128)}), f32[2,7,128]{2,1,0:T(8,128)}) %reduce-scatter.3.cloned.1.call-update) | async-done | bytes 7184 | tf_op jit(solution)/shard_map/reduce_scatter | solution.py:140
  107.4 0.8 fusion.31
  108.2 7.0 %fusion.60 = f32[14,32768]{1,0:T(8,128)} fusion(bf16[14,128]{1,0:T(8,128)(2,1)S(1)} %reshape.224, bf16[32768,128]{1,0:T(8,128)(2,1)} %param.13), kind=kOutput, calls=%fused_computation.106 | convolution fusion | flops 117440512 | bytes 10227200 | tf_op jit(solution)/shard_map/dot_general | solution.py:149
  115.4 0.6 copy.129
  116.0 19.6 %psum.31 = f32[2,7]{0,1:T(8,128)S(1)} all-reduce(f32[2,7]{0,1:T(8,128)S(1)} %copy.126), channel_id=1, replica_groups=mesh['seq'=4,'tensor'=8] {'tensor'}, use_global_device_ids=true, to_apply=%region_12.13 | all-reduce | flops 14 | bytes 112 | tf_op jit(solution)/shard_map/psum | solution.py:143
  135.6 0.6 copy.128
  136.2 0.1 copy.127
  136.4 46.6 %reduce-scatter.5.cloned.1.call-done = f32[14,4096]{1,0:T(8,128)} async-done(((f32[14,32768]{1,0:T(8,128)}), f32[14,4096]{1,0:T(8,128)}) %reduce-scatter.5.cloned.1.call-update) | async-done | bytes 229392 | tf_op jit(solution)/shard_map/reduce_scatter | solution.py:153
  183.0 1.2 multiply_reduce_fusion
  184.2 0.2 dynamic-update-slice
  184.4 1.2 exponential_reduce_fusion
  185.6 0.2 dynamic-update-slice.1
  185.8 39.5 %all-reduce.2 = (f32[448]{0:T(512)S(1)}, f32[448]{0:T(512)S(1)}) all-reduce(f32[448]{0:T(512)S(1)} %dynamic-update-slice, f32[448]{0:T(512)S(1)} %dynamic-update-slice.1), channel_id=2, replica_groups=mesh['seq'=4,'tensor'=8] {'seq','tensor'}, use_global_device_ids=true, to_apply=%add | all-reduce | flops 896 | bytes 7168
  225.5 0.1 reshape.243
  225.6 0.1 reshape.244
  225.7 1.2 while.12
  227.0 1.0 multiply_subtract_fusion
  228.1 0.9 copy.130
  (70 shorter events, 1.9 us)
Async XLA Ops:
  7.2 30.9 %copy-start = (bf16[7,1280,128]{2,1,0:T(8,128)(2,1)S(1)}, bf16[7,1280,128]{2,1,0:T(8,128)(2,1)}, u32[]{:S(2)}) copy-start(bf16[7,1280,128]{2,1,0:T(8,128)(2,1)} %param.18) | copy-start | bytes 6881284
  22.9 12.5 %all-to-all-start = ((bf16[8,2,7,128]{3,1,2,0:T(2,128)(2,1)}), bf16[8,2,7,128]{3,1,2,0:T(2,128)(2,1)S(1)}, u32[]{:S(2)}, u32[]{:S(2)}) async-start(bf16[8,2,7,128]{3,1,2,0:T(2,128)(2,1)} %stack.4), calls=%async_computation | async-start | bytes 57344 | tf_op jit(solution)/shard_map/all_to_all | solution.py:73
  28.7 78.7 %reduce-scatter.3.cloned.1.call-start = ((), (), s32[]{:S(2)}) async-start(), calls=%async_computation.3 | async-start | bytes 73728 | tf_op jit(solution)/shard_map/reduce_scatter | solution.py:140
  38.0 16.6 %copy-start.1 = (bf16[128,1024]{1,0:T(8,128)(2,1)S(1)}, bf16[128,1024]{1,0:T(8,128)(2,1)}, u32[]{:S(2)}) copy-start(bf16[128,1024]{1,0:T(8,128)(2,1)} %param.17) | copy-start | bytes 786436
  55.4 127.6 %reduce-scatter.5.cloned.1.call-start = ((), (), s32[]{:S(2)}) async-start(), calls=%async_computation.4 | async-start | bytes 2359296 | tf_op jit(solution)/shard_map/reduce_scatter | solution.py:153
Sparse Core Ops, SparseCore 0:
  55.6 51.7 reduce-scatter.2
  115.4 67.5 reduce-scatter.4
